TPU v7x, 32 devices: a whole 2x2x4 slice. The times are simulated.
32 devices in a mesh: groups: 2 (over x), tm: 8 (over z, y), sector: 2 (over core).
Axes of the slice: x: 2, y: 2, z: 4, core: 2. Of those that a mesh axis runs over, the one named last changes fastest.
Arguments:
- context: bfloat16 [16, 2, 512, 256], P(('groups', 'tm'), 'sector'), parts along dimension 0, may hold values from -6 to 6
- depth_weight: float32 [16, 2, 16, 512], P(('groups', 'tm'), 'sector'), parts along dimension 0, may hold values from 0 to 1
- cell_ids: int32 [2, 16, 512], P('sector'), may hold values from 0 to 4095
- time_embed: bfloat16 [8, 256], replicated, may hold values from -3 to 3
- norm_gain: float32 [2, 2, 256], replicated, may hold values from 0.1 to 1.9
- w_qkv: bfloat16 [2, 256, 768], replicated, may hold values from -15 to 15
- w_out: bfloat16 [2, 256, 256], replicated, may hold values from -0.375 to 0.375
- w_up: bfloat16 [2, 256, 1024], replicated, may hold values from -0.375 to 0.375
- w_down: bfloat16 [2, 1024, 256], replicated, may hold values from -0.1875 to 0.1875
- conv_weight: bfloat16 [3, 3, 256, 256], replicated, may hold values from -0.125 to 0.125
Outputs:
- bev_out: bfloat16 [16, 64, 64, 256], P(('groups', 'tm'), 'sector'), parts along dimension 0
There are 2 independent parts, one for each index of `groups`. A program takes and returns all parts, laid end to end along the dimension named above; an argument that names none is the same for every part. Nothing has to cross between parts.
All inputs are finite; a program needn't handle non-finite values.
Results may differ from a plain program's by a relative error of at most 0.0079.
Values may be sent and summed in bfloat16 or wider, within the bound.
No kernel may reach another device: no remote copies, remote signals or barrier semaphores. Data moves between devices by JAX's collectives and lax.ppermute only.
A program may use at most 128 MiB of HBM per device.

v0:
```python
import jax
import jax.numpy as jnp
from jax import lax
from jax.sharding import PartitionSpec as P

HEADS = 8
GRID = 64


def padded_2(cells, sides, width):
    for axis, dim in sides:
        count = lax.axis_size(axis)
        ends = count - 1
        head = lax.slice_in_dim(cells, 0, width, axis=dim)
        tail = lax.slice_in_dim(cells, cells.shape[dim] - width, cells.shape[dim], axis=dim)
        cells = jnp.concatenate(
            [
                lax.ppermute(tail, axis, [(i, (i + 1) % count) for i in range(ends)]),
                cells,
                lax.ppermute(head, axis, [((i + 1) % count, i) for i in range(ends)]),
            ],
            axis=dim,
        )
    return cells


def pool_local(context, depth_weight, cell_ids):
    cell_count = GRID * GRID
    block_cells = min(512, cell_count)
    cell_index = cell_ids[0]

    def one_frame(frame_inputs):
        features, weights = frame_inputs

        def one_block(first_cell):
            target = first_cell + lax.broadcasted_iota(jnp.int32, (block_cells, 1), 0)
            matches = cell_index[:, None, :] == target[None]
            matrix = jnp.sum(
                jnp.where(matches, weights[:, None, :], jnp.zeros_like(weights[:, None, :])), axis=0
            ).astype(jnp.bfloat16)
            return jnp.dot(matrix, features, preferred_element_type=jnp.float32).astype(
                jnp.bfloat16
            )

        starts = jnp.arange(cell_count // block_cells) * block_cells
        return lax.map(one_block, starts).reshape(cell_count, features.shape[-1])

    return lax.map(one_frame, (context[:, 0], depth_weight[:, 0]))


def normalize(values, gain):
    return values * lax.rsqrt(jnp.mean(values * values, axis=-1, keepdims=True) + 1e-05) * gain


def encode_stack(tokens, time_embed, norm_gain, w_qkv, w_out, w_up, w_down):
    frame_count, cell_count, channels = tokens.shape
    head_size = channels // HEADS
    query_frame = lax.broadcasted_iota(jnp.int32, (frame_count, frame_count), 0)
    key_frame = lax.broadcasted_iota(jnp.int32, (frame_count, frame_count), 1)
    allowed = key_frame <= query_frame
    stream = (tokens.astype(jnp.float32) + time_embed[:, None, :].astype(jnp.float32)).reshape(
        frame_count * cell_count, channels
    )
    for number in range(w_qkv.shape[0]):
        normed = normalize(stream, norm_gain[number, 0]).astype(jnp.bfloat16)
        projected = jnp.dot(normed, w_qkv[number], preferred_element_type=jnp.float32).astype(
            jnp.bfloat16
        )
        projected = projected.reshape(frame_count, cell_count, 3, HEADS, head_size)
        scores = jnp.einsum(
            "fchd,gchd->chfg",
            projected[:, :, 0],
            projected[:, :, 1],
            preferred_element_type=jnp.float32,
        ) * head_size ** (-0.5)
        scores = jnp.where(allowed, scores, -1e30)
        largest = jnp.max(scores, axis=-1, keepdims=True)
        raised = jnp.exp(scores - largest)
        soft_weights = (raised / jnp.sum(raised, axis=-1, keepdims=True)).astype(jnp.bfloat16)
        mixed = jnp.einsum(
            "chfg,gchd->fchd", soft_weights, projected[:, :, 2], preferred_element_type=jnp.float32
        ).astype(jnp.bfloat16)
        mixed = mixed.reshape(frame_count * cell_count, channels)
        stream = stream + jnp.dot(mixed, w_out[number], preferred_element_type=jnp.float32)
        normed_second = normalize(stream, norm_gain[number, 1]).astype(jnp.bfloat16)
        hidden_units = jax.nn.gelu(
            jnp.dot(normed_second, w_up[number], preferred_element_type=jnp.float32),
            approximate=True,
        ).astype(jnp.bfloat16)
        stream = stream + jnp.dot(hidden_units, w_down[number], preferred_element_type=jnp.float32)
    return stream.reshape(frame_count, cell_count, channels).astype(jnp.bfloat16)


def encode_return(tokens, weights):
    encoded = encode_stack(tokens, *weights)
    return lax.all_to_all(encoded, "tm", split_axis=0, concat_axis=1, tiled=True)


def body(
    context, depth_weight, cell_ids, time_embed, norm_gain, w_qkv, w_out, w_up, w_down, conv_weight
):
    partial_value = lax.optimization_barrier(pool_local(context, depth_weight, cell_ids))
    frames_dev, cell_count, channels = partial_value.shape
    tm_count = lax.axis_size("tm")
    band_cells = cell_count // lax.axis_size("sector")
    piece_cells = band_cells // tm_count
    weights = (time_embed, norm_gain, w_qkv, w_out, w_up, w_down)
    pooled = (
        lax.psum_scatter(partial_value, "sector", scatter_dimension=1, tiled=True)
        .astype(jnp.float32)
        .astype(jnp.bfloat16)
    )
    sectioned = pooled.reshape(frames_dev, tm_count, piece_cells, channels)
    received = lax.all_to_all(sectioned, "tm", split_axis=1, concat_axis=0, tiled=True)
    tokens = received.reshape(received.shape[0], received.shape[2], channels)
    returned = encode_return(tokens, weights)
    item_count = returned.shape[1] // tm_count
    result = returned.reshape(frames_dev, tm_count, item_count, channels)
    row_count = band_cells // GRID
    encoded = result.reshape(frames_dev, row_count, GRID, channels)
    padded = padded_2(encoded, (("sector", 1),), 1)
    padded = jnp.pad(padded, ((0, 0), (0, 0), (1, 1), (0, 0)))
    summed = encoded.astype(jnp.float32)
    for offset in range(3):
        row_strip = padded[:, offset : offset + row_count]
        stacked = jnp.concatenate(
            [row_strip[:, :, column : column + GRID] for column in range(3)], axis=-1
        )
        product = jnp.dot(
            stacked.reshape(frames_dev * row_count * GRID, 3 * channels),
            conv_weight[offset].reshape(3 * channels, channels),
            preferred_element_type=jnp.float32,
        )
        summed = summed + product.reshape(summed.shape)
    return summed.astype(jnp.bfloat16)


def solution(mesh):
    return jax.shard_map(
        body,
        mesh=mesh,
        in_specs=(
            P(("groups", "tm"), "sector", None, None),
            P(("groups", "tm"), "sector", None, None),
            P("sector", None, None),
            P(),
            P(),
            P(),
            P(),
            P(),
            P(),
            P(),
        ),
        out_specs=P(("groups", "tm"), "sector", None, None),
        check_vma=False,
    )
```

profile of v0, /device:TPU:0, one launch (start us, length us, event | category | flops | bytes accessed | tf_op | source)
XLA Modules:
  0.0 295.6 jit_solution(16586934135951967975)
XLA Ops:
  6.5 45.5 %while.17 = (s32[]{:T(128)}, bf16[8,512,256]{2,1,0:T(8,128)(2,1)}, s32[1,16,512]{2,1,0:T(8,128)}, s32[8]{0:T(128)S(1)}, f32[16,512]{1,0:T(8,128)}, /*index=5*/bf16[512,256]{1,0:T(8,128)(2,1)}, s32[]{:T(128)}) while((s32[]{:T(128)}, bf16[8,512,256]{2,1,0:T(8,128)(2,1)}, s32[1,16,512]{2,1,0:T(8,128)}, s32[8]{0:T(128)S(1)}, f32[16,512]{1,0:T(8,128)}, ...), condition=%wide.region_2.3_spmd, body=%wide.region_0.2_spmd.sunk | while | flops 146670080 | bytes 1643101 | solution.py:46
  52.0 12.6 %reduce-scatter.2.cloned.1.call-done = bf16[1,2048,256]{2,1,0:T(8,128)(2,1)} async-done(((bf16[1,4096,256]{2,1,0:T(8,128)(2,1)}), bf16[1,2048,256]{2,1,0:T(8,128)(2,1)}) %reduce-scatter.2.cloned.1.call-update) | async-done | bytes 1048592 | tf_op jit(solution)/shard_map/reduce_scatter | solution.py:109
  64.7 6.4 %all-to-all-start = ((bf16[1,8,256,256]{3,2,0,1:T(8,128)(2,1)}), bf16[1,8,256,256]{3,2,0,1:T(8,128)(2,1)S(1)}, u32[]{:S(2)}, u32[]{:S(2)}) async-start(bf16[1,8,256,256]{3,2,0,1:T(8,128)(2,1)} %bitcast.169), calls=%async_computation.1 | async-start | bytes 2097152 | tf_op jit(solution)/shard_map/all_to_all | solution.py:114
  71.2 26.0 %all-to-all-done = bf16[1,8,256,256]{3,2,0,1:T(8,128)(2,1)S(1)} async-done(((bf16[1,8,256,256]{3,2,0,1:T(8,128)(2,1)}), bf16[1,8,256,256]{3,2,0,1:T(8,128)(2,1)S(1)}, u32[]{:S(2)}, u32[]{:S(2)}) %all-to-all-start) | async-done | bytes 1048608 | tf_op jit(solution)/shard_map/all_to_all | solution.py:114
  106.3 7.2 %copy.70 = bf16[8,256,1,8,32]{4,0,3,1,2:T(8,128)(2,1)} copy(bf16[8,256,1,8,32]{1,0,4,3,2:T(8,128)(2,1)S(1)} %get-tuple-element.69) | data formatting | bytes 2097152
  113.5 7.2 %copy.71 = bf16[8,256,1,8,32]{4,0,3,1,2:T(8,128)(2,1)} copy(bf16[8,256,1,8,32]{1,0,4,3,2:T(8,128)(2,1)S(1)} %get-tuple-element.70) | data formatting | bytes 2097152
  120.7 9.0 %fusion.26 = f32[256,8,8,8]{2,3,1,0:T(8,128)} fusion(bf16[8,256,1,8,32]{4,0,3,1,2:T(8,128)(2,1)} %copy.71, bf16[8,256,1,8,32]{4,0,3,1,2:T(8,128)(2,1)} %copy.70), kind=kOutput, calls=%fused_computation.31 | convolution fusion | flops 8388608 | bytes 2621440 | tf_op jit(solution)/shard_map/fchd,gchd->chfg/dot_general | solution.py:70
  129.7 6.4 %copy.59 = f32[256,8,8,8]{0,3,2,1:T(8,128)S(1)} copy(f32[256,8,8,8]{2,3,1,0:T(8,128)} %fusion.26) | data formatting | bytes 1048576 | tf_op jit(solution)/shard_map/fchd,gchd->chfg/dot_general | solution.py:70
  137.1 6.4 %copy.60 = bf16[256,8,8,8]{3,2,1,0:T(8,128)(2,1)} copy(bf16[256,8,8,8]{0,3,2,1:T(8,128)(2,1)S(1)} %divide_convert_fusion.1) | data formatting | bytes 524288 | tf_op jit(solution)/shard_map/convert_element_type | solution.py:79
  143.5 7.4 %copy.69 = bf16[8,256,1,8,32]{4,0,3,1,2:T(8,128)(2,1)} copy(bf16[8,256,1,8,32]{1,0,4,3,2:T(8,128)(2,1)S(1)} %get-tuple-element.68) | data formatting | bytes 2097152
  150.9 7.8 %convert_bitcast_fusion.1 = bf16[8,256,8,32]{3,0,2,1:T(8,128)(2,1)} fusion(bf16[256,8,8,8]{3,2,1,0:T(8,128)(2,1)} %copy.60, bf16[8,256,1,8,32]{4,0,3,1,2:T(8,128)(2,1)} %copy.69), kind=kOutput, calls=%fused_computation.37 | convolution fusion | flops 8912896 | bytes 2359296 | tf_op jit(solution)/shard_map/chfg,gchd->fchd/dot_general | solution.py:80
  158.6 6.0 %copy.61 = bf16[8,256,8,32]{1,0,3,2:T(8,128)(2,1)S(1)} copy(bf16[8,256,8,32]{3,0,2,1:T(8,128)(2,1)} %convert_bitcast_fusion.1) | data formatting | bytes 2097152 | tf_op jit(solution)/shard_map/convert_element_type | solution.py:82
  166.3 5.9 %multiply_reduce_fusion.1 = (f32[2048]{0:T(1024)S(1)}, f32[2048,256]{1,0:T(8,128)}) fusion(f32[2048,256]{1,0:T(8,128)S(1)} %get-tuple-element.89, bf16[2,1024,256]{2,1,0:T(8,128)(2,1)} %param.20, f32[256]{0:T(256)S(1)} %bitcast.179, f32[2048]{0:T(1024)S(1)} %add_rsqrt_fusion.2, bf16[2,256,1024]{2,1,0:T(8,128)(2,1)} %param.19), kind=kOutput, calls=%fused_computation.83 | convolution fusion | flops 2169501696 | bytes 7357440 | tf_op jit(solution)/shard_map/dot_general | solution.py:90
  174.9 3.2 %copy.62 = bf16[2048,768]{0,1:T(8,128)(2,1)} copy(bf16[2048,768]{1,0:T(8,128)(2,1)S(1)} %convolution_convert_fusion.1) | data formatting | bytes 6291456 | tf_op jit(solution)/shard_map/convert_element_type | solution.py:66
  181.3 7.2 %copy.73 = bf16[8,256,1,8,32]{4,0,3,1,2:T(8,128)(2,1)} copy(bf16[8,256,1,8,32]{1,0,4,3,2:T(8,128)(2,1)S(1)} %get-tuple-element.66) | data formatting | bytes 2097152
  188.5 7.2 %copy.74 = bf16[8,256,1,8,32]{4,0,3,1,2:T(8,128)(2,1)} copy(bf16[8,256,1,8,32]{1,0,4,3,2:T(8,128)(2,1)S(1)} %get-tuple-element.67) | data formatting | bytes 2097152
  195.6 9.0 %fusion.21 = f32[256,8,8,8]{2,3,1,0:T(8,128)} fusion(bf16[8,256,1,8,32]{4,0,3,1,2:T(8,128)(2,1)} %copy.74, bf16[8,256,1,8,32]{4,0,3,1,2:T(8,128)(2,1)} %copy.73), kind=kOutput, calls=%fused_computation.26 | convolution fusion | flops 8388608 | bytes 2621440 | tf_op jit(solution)/shard_map/fchd,gchd->chfg/dot_general | solution.py:70
  204.6 6.4 %copy.66 = f32[256,8,8,8]{0,3,2,1:T(8,128)S(1)} copy(f32[256,8,8,8]{2,3,1,0:T(8,128)} %fusion.21) | data formatting | bytes 1048576 | tf_op jit(solution)/shard_map/fchd,gchd->chfg/dot_general | solution.py:70
  212.1 6.4 %copy.67 = bf16[256,8,8,8]{3,2,1,0:T(8,128)(2,1)} copy(bf16[256,8,8,8]{0,3,2,1:T(8,128)(2,1)S(1)} %divide_convert_fusion) | data formatting | bytes 524288 | tf_op jit(solution)/shard_map/convert_element_type | solution.py:79
  218.5 7.4 %copy.72 = bf16[8,256,1,8,32]{4,0,3,1,2:T(8,128)(2,1)} copy(bf16[8,256,1,8,32]{1,0,4,3,2:T(8,128)(2,1)S(1)} %get-tuple-element.65) | data formatting | bytes 2097152
  225.9 7.8 %convert_bitcast_fusion = bf16[8,256,8,32]{3,0,2,1:T(8,128)(2,1)} fusion(bf16[256,8,8,8]{3,2,1,0:T(8,128)(2,1)} %copy.67, bf16[8,256,1,8,32]{4,0,3,1,2:T(8,128)(2,1)} %copy.72), kind=kOutput, calls=%fused_computation.36 | convolution fusion | flops 8912896 | bytes 2359296 | tf_op jit(solution)/shard_map/chfg,gchd->fchd/dot_general | solution.py:80
  233.7 6.0 %copy.68 = bf16[8,256,8,32]{1,0,3,2:T(8,128)(2,1)S(1)} copy(bf16[8,256,8,32]{3,0,2,1:T(8,128)(2,1)} %convert_bitcast_fusion) | data formatting | bytes 2097152 | tf_op jit(solution)/shard_map/convert_element_type | solution.py:82
  242.0 5.6 %fusion.70 = bf16[2048,256]{1,0:T(8,128)(2,1)S(1)} fusion(f32[2048,256]{1,0:T(8,128)} %get-tuple-element.95, f32[256]{0:T(256)S(1)} %bitcast.178, f32[2048]{0:T(1024)S(1)} %add_rsqrt_fusion, bf16[2,1024,256]{2,1,0:T(8,128)(2,1)} %param.20, bf16[2,256,1024]{2,1,0:T(8,128)(2,1)} %param.19), kind=kOutput, calls=%fused_computation.72 | convolution fusion | flops 2168979456 | bytes 6300672 | tf_op jit(solution)/shard_map/dot_general | solution.py:90
  247.6 29.3 %all_to_all.8 = bf16[8,256,256]{2,1,0:T(8,128)(2,1)S(1)} all-to-all(bf16[8,256,256]{2,1,0:T(8,128)(2,1)S(1)} %bitcast.170), channel_id=1, replica_groups=mesh['groups'=2,'tm'=8,'sector'=2] {'tm'}, dimensions={0} | all-to-all | bytes 2097152 | tf_op jit(solution)/shard_map/all_to_all | solution.py:96
  (86 shorter events, 77.9 us)
Async XLA Ops:
  6.5 58.1 %reduce-scatter.2.cloned.1.call-start = ((), (), s32[]{:S(2)}) async-start(), calls=%async_computation.3 | async-start | bytes 3145728 | tf_op jit(solution)/shard_map/reduce_scatter | solution.py:109
  52.0 19.1 %copy-start.5 = (bf16[8,256]{1,0:T(8,128)(2,1)S(1)}, bf16[8,256]{1,0:T(8,128)(2,1)}, u32[]{:S(2)}) copy-start(bf16[8,256]{1,0:T(8,128)(2,1)} %param.15) | copy-start | bytes 12292
  52.0 19.1 %copy-start.6 = (f32[2,2,256]{2,1,0:T(2,128)S(1)}, f32[2,2,256]{2,1,0:T(2,128)}, u32[]{:S(2)}) copy-start(f32[2,2,256]{2,1,0:T(2,128)} %param.16) | copy-start | bytes 12292
  64.7 32.5 %all-to-all-start = ((bf16[1,8,256,256]{3,2,0,1:T(8,128)(2,1)}), bf16[1,8,256,256]{3,2,0,1:T(8,128)(2,1)S(1)}, u32[]{:S(2)}, u32[]{:S(2)}) async-start(bf16[1,8,256,256]{3,2,0,1:T(8,128)(2,1)} %bitcast.169), calls=%async_computation.1 | async-start | bytes 2097152 | tf_op jit(solution)/shard_map/all_to_all | solution.py:114
  97.2 1.0 copy-start
  158.6 6.3 %copy-start.1 = (bf16[1,8,256,256]{3,2,0,1:T(8,128)(2,1)S(1)}, bf16[1,8,256,256]{3,2,0,1:T(8,128)(2,1)}, u32[]{:S(2)}) copy-start(bf16[1,8,256,256]{3,2,0,1:T(8,128)(2,1)} %copy-done) | copy-start | bytes 3145732
  164.6 1.0 copy-start.4
  233.7 6.3 %copy-start.2 = (f32[2048,256]{1,0:T(8,128)S(1)}, f32[2048,256]{1,0:T(8,128)}, u32[]{:S(2)}) copy-start(f32[2048,256]{1,0:T(8,128)} %get-tuple-element.91) | copy-start | bytes 6291460
  242.0 37.6 %copy-start.3 = (bf16[3,3,256,256]{3,2,1,0:T(8,128)(2,1)S(1)}, bf16[3,3,256,256]{3,2,1,0:T(8,128)(2,1)}, u32[]{:S(2)}) copy-start(bf16[3,3,256,256]{3,2,1,0:T(8,128)(2,1)} %param.21) | copy-start | bytes 3538948
  277.0 2.7 collective-permute-start
  278.3 3.1 %collective-permute-start.1 = (bf16[1,1,64,256]{3,2,1,0:T(8,128)(2,1)S(1)}, bf16[1,1,64,256]{3,2,1,0:T(8,128)(2,1)S(1)}, u32[]{:S(2)}, u32[]{:S(2)}) collective-permute-start(bf16[1,1,64,256]{3,2,1,0:T(8,128)(2,1)S(1)} %get-tuple-element.81), channel_id=1, source_target_pairs={{1,0},{3,2},{5,4},{7,6},{9,8},{11,10},{13,12},{15,14},{17,16},{19,... | collective-permute-start | bytes 98312 | tf_op jit(solution)/shard_map/ppermute | solution.py:20
Sparse Core Ops, SparseCore 0:
  52.1 12.4 reduce-scatter.1
where the time goes:
time: 299 us; the launch traced here: 296 us
  local copies, waits for them, and re-layouts  101 us (34%)
  matrix products  73.3 us (25%)
  waiting for transfers between devices  40.3 us (13%)
  blocking collectives  29.3 us (10%)
  other arithmetic  28.7 us (10%)
  between operations  14 us (5%)
  starting transfers between devices  9.01 us (3%)
    unnamed x24, local copies, waits for them, and re-layouts  50.8 us
    all_to_all x1, blocking collectives, encode_return(): lax.all_to_all(encoded, 'tm', split_axis=0, concat_axis=1, tiled=True)  29.3 us
    all_to_all x1, waiting for transfers between devices, body(): lax.all_to_all(sectioned, 'tm', split_axis=1, concat_axis=0, tiled=True)  26 us
    reduce_sum x8, other arithmetic, one_block(): jnp.sum(jnp.where(matches, weights[:, None, :], jnp.zeros_like(weights[:,...  20 us
    dot_general x2, matrix products, encode_stack(): jnp.einsum('fchd,gchd->chfg', projected[:, :, 0], projected[:, :, 1], pre...  18 us
    dot_general x8, matrix products, one_block(): jnp.dot(matrix, features, preferred_element_type=jnp.float32)  15.7 us
    dot_general x2, matrix products, encode_stack(): jnp.einsum('chfg,gchd->fchd', soft_weights, projected[:, :, 2], preferred...  15.5 us
    convert_element_type x2, local copies, waits for them, and re-layouts, encode_stack(): (raised / jnp.sum(raised, axis=-1, keepdims=True)).astype(jnp.bfloat16)  12.8 us
  transfers between devices with their start and end apart: 4, of which 3 were waited for; matrix products, arithmetic and copies ran while one was open for 0% of the time, Pallas kernels for 0%

commit v1 on v0

v1 whole, which is shorter than its diff:
```python
import functools

import jax
import jax.numpy as jnp
from jax import lax
from jax.experimental import pallas as pl
from jax.experimental.pallas import tpu as pltpu
from jax.sharding import PartitionSpec as P

HEADS = 8
GRID = 64
LANES = 128
PACKED = 16
F32 = jnp.float32
BF16 = jnp.bfloat16
NT = (((1,), (1,)), ((), ()))


def padded_2(cells, sides, width):
    for axis, dim in sides:
        count = lax.axis_size(axis)
        ends = count - 1
        head = lax.slice_in_dim(cells, 0, width, axis=dim)
        tail = lax.slice_in_dim(cells, cells.shape[dim] - width, cells.shape[dim], axis=dim)
        cells = jnp.concatenate(
            [
                lax.ppermute(tail, axis, [(i, (i + 1) % count) for i in range(ends)]),
                cells,
                lax.ppermute(head, axis, [((i + 1) % count, i) for i in range(ends)]),
            ],
            axis=dim,
        )
    return cells


def pool_kernel(first_row, *refs):
    *sector_refs, out_ref, context_t, col_hot, row_id, matrix = refs
    sectors = len(sector_refs) // 3
    piece = pl.program_id(0)
    bins, pixels = sector_refs[1].shape
    rows = out_ref.shape[2] // GRID

    @pl.when(piece == 0)
    def _():
        for s in range(sectors):
            context, weight, ids = sector_refs[3 * s : 3 * s + 3]
            context_t[s] = context[...].astype(F32).T.astype(BF16)
            column = lax.broadcasted_iota(jnp.int32, (GRID, pixels), 0)
            for d in range(bins):
                cell = ids[d : d + 1, :]
                row = lax.div(cell, GRID)
                row_id[s, d] = jnp.broadcast_to(row.astype(F32), (PACKED, pixels)).astype(BF16)
                col_hot[s, d] = jnp.where(
                    column == cell - row * GRID, weight[d : d + 1, :], 0.0
                ).astype(BF16)

    for i in range(rows):
        target = (first_row[0] + piece * rows + i).astype(F32)
        target = jnp.full((PACKED, LANES), target, F32).astype(BF16)
        for s in range(sectors):
            for lane in range(0, pixels, LANES):
                at = slice(lane, lane + LANES)
                sums = [jnp.zeros((PACKED, LANES), BF16)] * (GRID // PACKED)
                for d in range(bins):
                    hit = row_id[s, d, :, at] == target
                    for j in range(GRID // PACKED):
                        part = col_hot[s, d, j * PACKED : (j + 1) * PACKED, at]
                        sums[j] = sums[j] + jnp.where(hit, part, jnp.zeros_like(part))
                for j in range(GRID // PACKED):
                    low = i * GRID + j * PACKED
                    matrix[s, low : low + PACKED, at] = sums[j]
    total = None
    for s in range(sectors):
        part = lax.dot_general(context_t[s], matrix[s], NT, preferred_element_type=F32)
        part = part.astype(BF16).astype(F32)
        total = part if total is None else total + part
    out_ref[0] = total.astype(BF16)


def pool(first_row, sector_args, pieces, piece_cells):
    pixels, channels = sector_args[0][0].shape
    bins = sector_args[0][1].shape[0]
    sectors = len(sector_args)
    whole = [pl.BlockSpec(memory_space=pltpu.VMEM)] * (3 * sectors)
    return pl.pallas_call(
        pool_kernel,
        grid=(pieces,),
        out_shape=jax.ShapeDtypeStruct((pieces, channels, piece_cells), BF16),
        in_specs=[pl.BlockSpec(memory_space=pltpu.SMEM)] + whole,
        out_specs=pl.BlockSpec((1, channels, piece_cells), lambda i: (i, 0, 0)),
        scratch_shapes=[
            pltpu.VMEM((sectors, channels, pixels), BF16),
            pltpu.VMEM((sectors, bins, GRID, pixels), BF16),
            pltpu.VMEM((sectors, bins, PACKED, pixels), BF16),
            pltpu.VMEM((sectors, piece_cells, pixels), BF16),
        ],
        compiler_params=pltpu.CompilerParams(dimension_semantics=("arbitrary",)),
        cost_estimate=pl.CostEstimate(
            flops=2 * sectors * pieces * piece_cells * pixels * channels,
            bytes_accessed=2 * pieces * piece_cells * channels,
            transcendentals=0,
        ),
        name="pool",
    )(first_row, *[a for args in sector_args for a in args])


def prep_kernel(w_qkv, w_out, w_up, w_down, qkv_t, out_t, up_t, down_t):
    layers, channels, _ = w_qkv.shape
    hidden = w_up.shape[2]
    size = channels // HEADS
    row = lax.broadcasted_iota(jnp.int32, (channels, channels), 0)
    col = lax.broadcasted_iota(jnp.int32, (channels, channels), 1)
    order = (col == (row % HEADS) * size + row // HEADS).astype(F32).astype(BF16)
    same = (col == row).astype(F32).astype(BF16)

    def turned(left, right):
        return lax.dot_general(left, right, NT, preferred_element_type=F32).astype(BF16)

    for l in range(layers):
        for j in range(3):
            at = slice(j * channels, (j + 1) * channels)
            qkv_t[l, at, :] = turned(order, w_qkv[l, :, at])
        rows = jnp.dot(order, w_out[l], preferred_element_type=F32).astype(BF16)
        out_t[l] = turned(same, rows)
        for j in range(0, hidden, channels):
            at = slice(j, j + channels)
            up_t[l, at, :] = turned(same, w_up[l, :, at])
            down_t[l, :, at] = turned(same, w_down[l, at, :])


def prep(w_qkv, w_out, w_up, w_down):
    turned = lambda w: jax.ShapeDtypeStruct((w.shape[0], w.shape[2], w.shape[1]), w.dtype)
    return pl.pallas_call(
        prep_kernel,
        out_shape=[turned(w) for w in (w_qkv, w_out, w_up, w_down)],
        in_specs=[pl.BlockSpec(memory_space=pltpu.VMEM)] * 4,
        out_specs=[pl.BlockSpec(memory_space=pltpu.VMEM)] * 4,
        name="prep",
    )(w_qkv, w_out, w_up, w_down)


def normed_tile(stream, gain):
    mean = jnp.mean(stream * stream, axis=0, keepdims=True)
    scale = lax.rsqrt(mean + 1e-05)
    lanes = stream.shape[1]
    gains = jnp.concatenate([gain] * (lanes // LANES), axis=1)
    return (stream * scale * gains).astype(BF16)


def query_groups(frames, most):
    groups, group, pairs = [], [], 0
    for f in range(frames):
        if group and pairs + f + 1 > most:
            groups.append(group)
            group, pairs = [], 0
        group.append(f)
        pairs += f + 1
    return groups + [group]


def attention(qkv, mixed, frames, cells, channels):
    size = channels // HEADS
    for group in query_groups(frames, 40):
        last = group[-1]
        for lane in range(0, cells, LANES):
            pairs = [(f, g) for f in group for g in range(f + 1)]

            def at(f):
                return slice(f * cells + lane, f * cells + lane + LANES)

            def score_step(d, sums):
                row = pl.multiple_of(d * HEADS, HEADS)
                query = {f: qkv[pl.ds(row, HEADS), at(f)] for f in group}
                keys = [qkv[pl.ds(channels + row, HEADS), at(g)] for g in range(last + 1)]
                return tuple(s + query[f] * keys[g] for s, (f, g) in zip(sums, pairs))

            zeros = tuple(jnp.zeros((HEADS, LANES), F32) for _ in pairs)
            scores = dict(zip(pairs, lax.fori_loop(0, size, score_step, zeros, unroll=4)))
            weights = {}
            for f in group:
                row = [scores[f, g] for g in range(f + 1)]
                largest = functools.reduce(jnp.maximum, row)
                raised = [jnp.exp((s - largest) * size ** (-0.5)) for s in row]
                share = 1.0 / functools.reduce(jnp.add, raised)
                for g in range(f + 1):
                    weights[f, g] = (raised[g] * share).astype(BF16).astype(F32)

            def mix_step(step, carry):
                parts = {f: [] for f in group}
                for half in range(2):
                    row = pl.multiple_of(2 * channels + (2 * step + half) * HEADS, HEADS)
                    values = [qkv[pl.ds(row, HEADS), at(g)] for g in range(last + 1)]
                    for f in group:
                        terms = [carry[pairs.index((f, g))] * values[g] for g in range(f + 1)]
                        parts[f].append(functools.reduce(jnp.add, terms))
                low = pl.multiple_of(step * 2 * HEADS, 2 * HEADS)
                for f in group:
                    mixed[pl.ds(low, 2 * HEADS), at(f)] = jnp.concatenate(
                        parts[f], axis=0
                    ).astype(BF16)
                return carry

            lax.fori_loop(
                0, size // 2, mix_step, tuple(weights[pair] for pair in pairs), unroll=2
            )


def encode_kernel(
    tokens, embed, gains, qkv_t, out_t, up_t, down_t, encoded, stream, qkv, mixed, *, tile
):
    frames, channels, cells = tokens.shape
    layers = qkv_t.shape[0]
    lanes = frames * cells
    for f in range(frames):
        for lane in range(0, cells, LANES):
            stream[:, f * cells + lane : f * cells + lane + LANES] = (
                tokens[f, :, lane : lane + LANES].astype(F32) + embed[f]
            )

    def layer(l, _):
        def project(t, _):
            at = pl.ds(pl.multiple_of(t * tile, tile), tile)
            normed = normed_tile(stream[:, at], gains[l, 0])
            out = jnp.dot(qkv_t[l], normed, preferred_element_type=F32)
            qkv[:, at] = out.astype(BF16).astype(F32)
            return 0

        lax.fori_loop(0, lanes // tile, project, 0)
        attention(qkv, mixed, frames, cells, channels)

        def feed(t, _):
            at = pl.ds(pl.multiple_of(t * tile, tile), tile)
            current = stream[:, at] + jnp.dot(
                out_t[l], mixed[:, at], preferred_element_type=F32
            )
            normed = normed_tile(current, gains[l, 1])
            up = jnp.dot(up_t[l], normed, preferred_element_type=F32)
            hidden = jax.nn.gelu(up, approximate=True).astype(BF16)
            stream[:, at] = current + jnp.dot(down_t[l], hidden, preferred_element_type=F32)
            return 0

        lax.fori_loop(0, lanes // tile, feed, 0)
        return 0

    lax.fori_loop(0, layers, layer, 0)
    for f in range(frames):
        encoded[f] = stream[:, f * cells : (f + 1) * cells].T.astype(BF16)


def encode(tokens, embed, gains, weights):
    frames, channels, cells = tokens.shape
    layers, hidden = weights[2].shape[:2]
    lanes = frames * cells
    tile = min(lanes, 512)
    count = frames * cells
    return pl.pallas_call(
        functools.partial(encode_kernel, tile=tile),
        out_shape=jax.ShapeDtypeStruct((frames, cells, channels), BF16),
        in_specs=[pl.BlockSpec(memory_space=pltpu.VMEM)] * 7,
        out_specs=pl.BlockSpec(memory_space=pltpu.VMEM),
        scratch_shapes=[
            pltpu.VMEM((channels, lanes), F32),
            pltpu.VMEM((3 * channels, lanes), F32),
            pltpu.VMEM((channels, lanes), BF16),
        ],
        cost_estimate=pl.CostEstimate(
            flops=2 * layers * count * channels * (4 * channels + 2 * hidden),
            bytes_accessed=4 * count * channels,
            transcendentals=layers * count * hidden,
        ),
        name="encode",
    )(tokens, embed, gains, *weights)


def body(
    context, depth_weight, cell_ids, time_embed, norm_gain, w_qkv, w_out, w_up, w_down, conv_weight
):
    sector_count = lax.axis_size("sector")
    tm_count = lax.axis_size("tm")
    frames_dev, _, _, channels = context.shape
    band_cells = GRID * GRID // sector_count
    piece_cells = band_cells // tm_count
    row_count = band_cells // GRID

    def from_others(value):
        values = [value]
        for shift in range(1, sector_count):
            ring = [(i, (i + shift) % sector_count) for i in range(sector_count)]
            values.append(lax.ppermute(value, "sector", ring))
        return values

    contexts, depths, ids = map(from_others, (context[:, 0], depth_weight[:, 0], cell_ids[0]))
    first_row = (lax.axis_index("sector") * row_count).astype(jnp.int32).reshape(1)
    weights = prep(w_qkv, w_out, w_up, w_down)
    embed = jnp.broadcast_to(time_embed.astype(F32)[:, :, None], time_embed.shape + (LANES,))
    gains = jnp.broadcast_to(norm_gain[..., None], norm_gain.shape + (LANES,))
    pooled = jnp.stack(
        [
            pool(
                first_row,
                [(c[n], w[n], i) for c, w, i in zip(contexts, depths, ids)],
                tm_count,
                piece_cells,
            )
            for n in range(frames_dev)
        ]
    )
    received = lax.all_to_all(pooled, "tm", split_axis=1, concat_axis=0, tiled=True)
    tokens = received.reshape(frames_dev * tm_count, channels, piece_cells)
    spare = -piece_cells % LANES
    tokens = jnp.pad(tokens, ((0, 0), (0, 0), (0, spare)))
    encoded = encode(tokens, embed, gains, weights)[:, :piece_cells]
    encoded = encoded.reshape(tm_count, frames_dev, piece_cells, channels)
    encoded = encoded.transpose(1, 0, 2, 3)
    returned = lax.all_to_all(encoded, "tm", split_axis=1, concat_axis=0, tiled=True)
    returned = returned.reshape(tm_count, frames_dev, piece_cells, channels).transpose(1, 0, 2, 3)
    encoded = returned.reshape(frames_dev, row_count, GRID, channels)
    padded = padded_2(encoded, (("sector", 1),), 1)
    padded = jnp.pad(padded, ((0, 0), (0, 0), (1, 1), (0, 0)))
    summed = encoded.astype(F32)
    for offset in range(3):
        row_strip = padded[:, offset : offset + row_count]
        stacked = jnp.concatenate(
            [row_strip[:, :, column : column + GRID] for column in range(3)], axis=-1
        )
        product = jnp.dot(
            stacked.reshape(frames_dev * row_count * GRID, 3 * channels),
            conv_weight[offset].reshape(3 * channels, channels),
            preferred_element_type=F32,
        )
        summed = summed + product.reshape(summed.shape)
    return summed.astype(BF16)


def solution(mesh):
    return jax.shard_map(
        body,
        mesh=mesh,
        in_specs=(
            P(("groups", "tm"), "sector", None, None),
            P(("groups", "tm"), "sector", None, None),
            P("sector", None, None),
            P(),
            P(),
            P(),
            P(),
            P(),
            P(),
            P(),
        ),
        out_specs=P(("groups", "tm"), "sector", None, None),
        check_vma=False,
    )
```

time: 299 us -> 122 us (0.41); the launches traced: 296 us -> 122 us
  local copies, waits for them, and re-layouts: 101 us -> 4.38 us
  matrix products: 73.3 us -> 5.23 us
  Pallas kernels: 0 us -> 46.8 us
  other arithmetic: 28.7 us -> 0.68 us
  waiting for transfers between devices: 40.3 us -> 24.3 us
  between operations: 14 us -> 0.08 us
    dot_general x18 -> x0, matrix products: 68 us -> none  [the longest x2 18 us: encode_stack(): jnp.einsum('fchd,gchd->chfg', projected[:, :, 0], projected[:, :, 1], pre...]
    unnamed x24 -> x14, local copies, waits for them, and re-layouts: 50.8 us -> 0.73 us
    pallas_call x0 -> x3, Pallas kernels: none -> 46.8 us  [the longest x1 21.9 us: encode(): pl.pallas_call(functools.partial(encode_kernel, tile=tile), out_shape=jax...]
    convert_element_type x6 -> x0, local copies, waits for them, and re-layouts: 31 us -> none  [the longest x2 12.8 us: encode_stack(): (raised / jnp.sum(raised, axis=-1, keepdims=True)).astype(jnp.bfloat16)]
    reduce_sum x9 -> x0, other arithmetic: 20.3 us -> none  [the longest x8 20 us: one_block(): jnp.sum(jnp.where(matches, weights[:, None, :], jnp.zeros_like(weights[:,...]
    dot_general x2 -> x0, local copies, waits for them, and re-layouts: 12.7 us -> none  [encode_stack(): jnp.einsum('fchd,gchd->chfg', projected[:, :, 0], projected[:, :, 1], pre...]
    reduce_scatter x1 -> x0, waiting for transfers between devices: 12.6 us -> none  [body(): lax.psum_scatter(partial_value, 'sector', scatter_dimension=1, tiled=True)]
    add x9 -> x0, other arithmetic: 5.08 us -> none  [the longest x8 4.94 us: one_block(): target = first_cell + lax.broadcasted_iota(jnp.int32, (block_cells, 1), 0)]
  transfers between devices with their start and end apart: 4 -> 6, of which waited for: 3 -> 4; matrix products, arithmetic and copies ran while one was open for 0% -> 0% of each run, Pallas kernels for 0% -> 4%
where the time goes in v1:
time: 122 us
  Pallas kernels  46.8 us (38%)
  blocking collectives  29.7 us (24%)
  waiting for transfers between devices  24.3 us (20%)
  starting transfers between devices  10.9 us (9%)
  matrix products  5.23 us (4%)
  local copies, waits for them, and re-layouts  4.38 us (4%)
    all_to_all x1, blocking collectives, body(): lax.all_to_all(encoded, 'tm', split_axis=1, concat_axis=0, tiled=True)  29.7 us
    pallas_call x1, Pallas kernels, encode(): pl.pallas_call(functools.partial(encode_kernel, tile=tile), out_shape=jax...  21.9 us
    all_to_all x1, waiting for transfers between devices, body(): lax.all_to_all(pooled, 'tm', split_axis=1, concat_axis=0, tiled=True)  21.6 us
    pallas_call x1, Pallas kernels, pool(): pl.pallas_call(pool_kernel, grid=(pieces,), out_shape=jax.ShapeDtypeStruc...  20.4 us
    all_to_all x1, starting transfers between devices, body(): lax.all_to_all(pooled, 'tm', split_axis=1, concat_axis=0, tiled=True)  7.29 us
    dot_general x3, matrix products, body(): jnp.dot(stacked.reshape(frames_dev * row_count * GRID, 3 * channels), con...  5.23 us
    pallas_call x1, Pallas kernels, prep(): pl.pallas_call(prep_kernel, out_shape=[turned(w) for w in (w_qkv, w_out,...  4.53 us
  transfers between devices with their start and end apart: 6, of which 4 were waited for; matrix products, arithmetic and copies ran while one was open for 0% of the time, Pallas kernels for 4%

profile of v1, /device:TPU:0, one launch (start us, length us, event | category | flops | bytes accessed | tf_op | source)
XLA Modules:
  0.0 122.1 jit_solution(16193401947283457324)
XLA Ops:
  0.0 0.5 collective-permute-start
  0.5 0.5 collective-permute-start.1
  1.0 0.9 collective-permute-done.2.refs_5_
  1.9 0.2 collective-permute-done.1
  2.1 0.4 copy-done.5
  2.5 0.2 copy-done.6
  2.7 0.1 copy-done.4
  2.8 20.4 %pool.1 = bf16[8,256,256]{2,1,0:T(8,128)(2,1)} custom-call(s32[1]{0:T(128)} %bitcast.first_row, bf16[512,256]{1,0:T(8,128)(2,1)} %bitcast.58, f32[16,512]{1,0:T(8,128)} %bitcast.61, s32[16,512]{1,0:T(8,128)} %bitcast.63, bf16[512,256]{1,0:T(8,128)(2,1)} %bitcast.59, f32[16,512]{1,0:T(8,128)} %bitcast.64, s32[16,512]{1,0:T(8,128)} %copy-done.5), custom_call_target="tpu_custom_call" | custom-call | flops 1073741824 | bytes 1048576 | tf_op jit(solution)/shard_map/pool/pallas_call | solution.py:85
  23.2 7.3 %all-to-all-start = ((bf16[1,8,256,256]{3,2,0,1:T(8,128)(2,1)}), bf16[1,8,256,256]{3,2,0,1:T(8,128)(2,1)S(1)}, u32[]{:S(2)}, u32[]{:S(2)}) async-start(bf16[1,8,256,256]{3,2,0,1:T(8,128)(2,1)} %bitcast.52), calls=%async_computation | async-start | bytes 2097152 | tf_op jit(solution)/shard_map/all_to_all | solution.py:308
  30.5 4.5 %prep.1 = (bf16[2,768,256]{2,1,0:T(8,128)(2,1)}, bf16[2,256,256]{2,1,0:T(8,128)(2,1)}, bf16[2,1024,256]{2,1,0:T(8,128)(2,1)}, bf16[2,256,1024]{2,1,0:T(8,128)(2,1)}) custom-call(bf16[2,256,768]{2,1,0:T(8,128)(2,1)} %w_qkv.1, bf16[2,256,256]{2,1,0:T(8,128)(2,1)} %w_out.1, bf16[2,256,1024]{2,1,0:T(8,128)(2,1)} %w_up.1, bf16[2,1024,256]{2,1,0:T(8,128)(2,1)} %w_down.1), custom_call_target="tpu_custom_call" | custom-call | tf_op jit(solution)/shard_map/prep/pallas_call | solution.py:133
  35.1 21.6 %all-to-all-done = bf16[1,8,256,256]{3,2,0,1:T(8,128)(2,1)S(1)} async-done(((bf16[1,8,256,256]{3,2,0,1:T(8,128)(2,1)}), bf16[1,8,256,256]{3,2,0,1:T(8,128)(2,1)S(1)}, u32[]{:S(2)}, u32[]{:S(2)}) %all-to-all-start) | async-done | bytes 1048608 | tf_op jit(solution)/shard_map/all_to_all | solution.py:308
  56.6 1.2 broadcast_in_dim.5.gains
  57.8 1.3 %broadcast_in_dim.4.embed = f32[8,256,128]{2,1,0:T(8,128)} broadcast(bf16[8,256]{1,0:T(8,128)(2,1)S(1)} %copy-done.3), dimensions={0,1} | broadcast | bytes 1052672 | tf_op jit(solution)/shard_map/broadcast_in_dim | solution.py:295
  59.1 21.9 %encode.1 = bf16[8,256,256]{2,1,0:T(8,128)(2,1)} custom-call(bf16[8,256,256]{2,1,0:T(8,128)(2,1)} %bitcast.51, f32[8,256,128]{2,1,0:T(8,128)} %broadcast_in_dim.4.embed, f32[2,2,256,128]{3,2,1,0:T(8,128)} %broadcast_in_dim.5.gains, bf16[2,768,256]{2,1,0:T(8,128)(2,1)} %get-tuple-element.9.qkv_t, bf16[2,256,256]{2,1,0:T(8,128)(2,1)} %get-tuple-element.10.out_t, ...), custom_call_target="tpu_custom_call" | custom-call | flops 6442450944 | bytes 2097152 | tf_op jit(solution)/shard_map/encode/pallas_call | solution.py:256
  81.0 29.7 %all_to_all.8 = bf16[1,8,256,256]{3,2,0,1:T(8,128)(2,1)S(1)} all-to-all(bf16[1,8,256,256]{3,2,0,1:T(8,128)(2,1)} %bitcast.53), channel_id=1, replica_groups=mesh['groups'=2,'tm'=8,'sector'=2] {'tm'}, dimensions={1} | all-to-all | bytes 2097152 | tf_op jit(solution)/shard_map/all_to_all | solution.py:315
  110.7 1.3 %collective-permute-start.3 = (bf16[1,1,64,256]{3,2,1,0:T(8,128)(2,1)S(1)}, bf16[1,1,64,256]{3,2,1,0:T(8,128)(2,1)S(1)}, u32[]{:S(2)}, u32[]{:S(2)}) collective-permute-start(bf16[1,1,64,256]{3,2,1,0:T(8,128)(2,1)S(1)} %get-tuple-element.22), channel_id=1, source_target_pairs={{0,1},{2,3},{4,5},{6,7},{8,9},{10,11},{12,13},{14,15},{16,17},{18,... | collective-permute-start | bytes 98312 | tf_op jit(solution)/shard_map/ppermute | solution.py:27
  111.9 1.3 %collective-permute-start.4 = (bf16[1,1,64,256]{3,2,1,0:T(8,128)(2,1)S(1)}, bf16[1,1,64,256]{3,2,1,0:T(8,128)(2,1)S(1)}, u32[]{:S(2)}, u32[]{:S(2)}) collective-permute-start(bf16[1,1,64,256]{3,2,1,0:T(8,128)(2,1)S(1)} %get-tuple-element.23), channel_id=1, source_target_pairs={{1,0},{3,2},{5,4},{7,6},{9,8},{11,10},{13,12},{15,14},{17,16},{19,... | collective-permute-start | bytes 98312 | tf_op jit(solution)/shard_map/ppermute | solution.py:29
  113.3 0.1 fusion.39
  113.4 1.7 %collective-permute-done.4 = bf16[1,1,64,256]{3,2,1,0:T(8,128)(2,1)S(1)} collective-permute-done((bf16[1,1,64,256]{3,2,1,0:T(8,128)(2,1)S(1)}, bf16[1,1,64,256]{3,2,1,0:T(8,128)(2,1)S(1)}, u32[]{:S(2)}, u32[]{:S(2)}) %collective-permute-start.4) | collective-permute-done | bytes 32800 | tf_op jit(solution)/shard_map/ppermute | solution.py:29
  115.0 0.7 fusion.34
  115.7 1.1 fusion.38
  116.8 1.6 %fusion.14 = f32[32,64,256]{2,1,0:T(8,128)S(1)} fusion(bf16[768,256,1]{1,0,2:T(8,128)(2,1)S(1)} %bitcast.56, bf16[1,32,64,256]{3,2,1,0:T(8,128)(2,1)S(1)} %get-tuple-element.15, bf16[1,32,64,256]{3,2,1,0:T(8,128)(2,1)S(1)} %bitcast.47, bf16[1,32,64,256]{3,2,1,0:T(8,128)(2,1)S(1)} %get-tuple-element.16), kind=kOutput, calls=%fused_computation.17 | convolution fusion | flops 814743552 | bytes 5636096 | tf_op jit(solution)/shard_map/dot_general | solution.py:326
  118.4 1.6 %fusion.9 = f32[32,64,256]{2,1,0:T(8,128)S(1)} fusion(bf16[768,256,1]{1,0,2:T(8,128)(2,1)S(1)} %bitcast.55, bf16[1,32,64,256]{3,2,1,0:T(8,128)(2,1)S(1)} %bitcast.48, bf16[1,1,64,256]{3,2,1,0:T(8,128)(2,1)S(1)} %collective-permute-done.3, bf16[1,32,64,256]{3,2,1,0:T(8,128)(2,1)S(1)} %get-tuple-element.17, bf16[1,32,64,256]{3,2,1,0:T(8,128)(2,1)S(1)} %get-tuple-element.13), kind=kOutput, calls=%fused_computation.12 | convolution fusion | flops 817889280 | bytes 5668864 | tf_op jit(solution)/shard_map/dot_general | solution.py:326
  120.0 2.1 %fusion.30 = bf16[1,32,64,256]{3,2,1,0:T(8,128)(2,1)} fusion(bf16[768,256,1]{1,0,2:T(8,128)(2,1)S(1)} %bitcast.54, bf16[1,1,64,256]{3,2,1,0:T(8,128)(2,1)S(1)} %collective-permute-done.4, bf16[1,32,64,256]{3,2,1,0:T(8,128)(2,1)S(1)} %bitcast.49, bf16[1,32,64,256]{3,2,1,0:T(8,128)(2,1)S(1)} %get-tuple-element.18, ...), kind=kOutput, calls=%fused_computation.32 | convolution fusion | flops 820510720 | bytes 9863168 | tf_op jit(solution)/shard_map/dot_general | solution.py:326
  (15 shorter events, 0.0 us)
Async XLA Ops:
  0.0 2.1 %collective-permute-start = (bf16[1,512,256]{2,1,0:T(8,128)(2,1)}, bf16[1,512,256]{2,1,0:T(8,128)(2,1)S(1)}, u32[]{:S(2)}, u32[]{:S(2)}) collective-permute-start(bf16[1,512,256]{2,1,0:T(8,128)(2,1)} %bitcast.57), channel_id=1, source_target_pairs={{0,1},{1,0},{2,3},{3,2},{4,5},{5,4},{6,7},{7,6},{8,9},{9,8},{10,11... | collective-permute-start | bytes 786440 | tf_op jit(solution)/shard_map/ppermute | solution.py:289
  0.5 1.4 %collective-permute-start.2 = (s32[16,512]{1,0:T(8,128)}, s32[16,512]{1,0:T(8,128)S(1)}, u32[]{:S(2)}, u32[]{:S(2)}) collective-permute-start(s32[16,512]{1,0:T(8,128)} %bitcast.62), channel_id=1, source_target_pairs={{0,1},{1,0},{2,3},{3,2},{4,5},{5,4},{6,7},{7,6},{8,9},{9,8},{10,11... | collective-permute-start | bytes 98312 | tf_op jit(solution)/shard_map/ppermute | solution.py:289
  0.5 1.6 %collective-permute-start.1 = (f32[1,16,512]{2,1,0:T(8,128)}, f32[1,16,512]{2,1,0:T(8,128)S(1)}, u32[]{:S(2)}, u32[]{:S(2)}) collective-permute-start(f32[1,16,512]{2,1,0:T(8,128)} %bitcast.60), channel_id=1, source_target_pairs={{0,1},{1,0},{2,3},{3,2},{4,5},{5,4},{6,7},{7,6},{8,9},{9,8},{10,11... | collective-permute-start | bytes 98312 | tf_op jit(solution)/shard_map/ppermute | solution.py:289
  1.9 0.6 copy-start.5
  2.1 0.6 copy-start.6
  2.1 0.7 copy-start.4
  23.2 33.4 %copy-start.2 = (f32[2,2,256]{2,1,0:T(2,128)S(1)}, f32[2,2,256]{2,1,0:T(2,128)}, u32[]{:S(2)}) copy-start(f32[2,2,256]{2,1,0:T(2,128)} %param.14) | copy-start | bytes 12292
  23.2 33.4 %all-to-all-start = ((bf16[1,8,256,256]{3,2,0,1:T(8,128)(2,1)}), bf16[1,8,256,256]{3,2,0,1:T(8,128)(2,1)S(1)}, u32[]{:S(2)}, u32[]{:S(2)}) async-start(bf16[1,8,256,256]{3,2,0,1:T(8,128)(2,1)} %bitcast.52), calls=%async_computation | async-start | bytes 2097152 | tf_op jit(solution)/shard_map/all_to_all | solution.py:308
  30.5 27.3 %copy-start.3 = (bf16[8,256]{1,0:T(8,128)(2,1)S(1)}, bf16[8,256]{1,0:T(8,128)(2,1)}, u32[]{:S(2)}) copy-start(bf16[8,256]{1,0:T(8,128)(2,1)} %param.13) | copy-start | bytes 12292
  56.6 2.5 %copy-start.1 = (bf16[1,8,256,256]{3,2,0,1:T(8,128)(2,1)}, bf16[1,8,256,256]{3,2,0,1:T(8,128)(2,1)S(1)}, u32[]{:S(2)}) copy-start(bf16[1,8,256,256]{3,2,0,1:T(8,128)(2,1)S(1)} %all-to-all-done) | copy-start | bytes 3145732
  81.0 32.3 %copy-start = (bf16[3,3,256,256]{3,2,1,0:T(8,128)(2,1)S(1)}, bf16[3,3,256,256]{3,2,1,0:T(8,128)(2,1)}, u32[]{:S(2)}) copy-start(bf16[3,3,256,256]{3,2,1,0:T(8,128)(2,1)} %param.19) | copy-start | bytes 3538948
  110.7 2.7 %collective-permute-start.3 = (bf16[1,1,64,256]{3,2,1,0:T(8,128)(2,1)S(1)}, bf16[1,1,64,256]{3,2,1,0:T(8,128)(2,1)S(1)}, u32[]{:S(2)}, u32[]{:S(2)}) collective-permute-start(bf16[1,1,64,256]{3,2,1,0:T(8,128)(2,1)S(1)} %get-tuple-element.22), channel_id=1, source_target_pairs={{0,1},{2,3},{4,5},{6,7},{8,9},{10,11},{12,13},{14,15},{16,17},{18,... | collective-permute-start | bytes 98312 | tf_op jit(solution)/shard_map/ppermute | solution.py:27
  111.9 3.1 %collective-permute-start.4 = (bf16[1,1,64,256]{3,2,1,0:T(8,128)(2,1)S(1)}, bf16[1,1,64,256]{3,2,1,0:T(8,128)(2,1)S(1)}, u32[]{:S(2)}, u32[]{:S(2)}) collective-permute-start(bf16[1,1,64,256]{3,2,1,0:T(8,128)(2,1)S(1)} %get-tuple-element.23), channel_id=1, source_target_pairs={{1,0},{3,2},{5,4},{7,6},{9,8},{11,10},{13,12},{15,14},{17,16},{19,... | collective-permute-start | bytes 98312 | tf_op jit(solution)/shard_map/ppermute | solution.py:29
